TPU v7x, 32 devices: a whole 2x2x4 slice. The times are simulated.
32 devices in a mesh: dp: 4 (over x, core), pipe: 2 (over y), tensor: 4 (over z).
Axes of the slice: x: 2, y: 2, z: 4, core: 2. Of those that a mesh axis runs over, the one named last changes fastest.
Arguments:
- weights: bfloat16 [2816, 1408], P(('dp', 'pipe', 'tensor')), may hold values from -6 to 6
- first_moment: bfloat16 [2816, 1408], P(('dp', 'pipe', 'tensor')), may hold values from -6 to 6
- second_moment: bfloat16 [2816, 1408], P(('dp', 'pipe', 'tensor')), may hold values from 0.049804688 to 5
- row_weight: float32 [1408], replicated, may hold values from -1 to 1
- col_weight: float32 [1408], replicated, may hold values from 1 to 4
Outputs:
- weight_tiles: bfloat16 [2816, 1408], P(('pipe', 'tensor'))
- first_tiles: bfloat16 [2816, 1408], P(('pipe', 'tensor'))
- second_tiles: bfloat16 [2816, 1408], P(('pipe', 'tensor'))
- checksums: float32 [3, 2, 4, 11], P(None, 'pipe', 'tensor')
All inputs are finite; a program needn't handle non-finite values.
Results may differ from a plain program's by a relative error of at most 0.001.
Values may be sent and summed in bfloat16 or wider, within the bound.
No kernel may reach another device: no remote copies, remote signals or barrier semaphores. Data moves between devices by JAX's collectives and lax.ppermute only.
A program may use at most 64 MiB of HBM per device.

v0:
```python
import jax
import jax.numpy as jnp
from jax import lax
from jax.sharding import PartitionSpec as P

CHECK_COLS = 128


def for_sending(array):
    return jax.tree.map(lambda a: a.astype(jnp.bfloat16) if a.dtype == jnp.float32 else a, array)


def column_sums(data, row_part, col_weight, col_blocks):
    row_mixed = jnp.dot(
        row_part[None, :], data.astype(jnp.float32), precision=lax.Precision.HIGHEST
    )[0]
    return jnp.sum((row_mixed * col_weight).reshape(col_blocks, -1), axis=1)


def shards(weights, first_moment, second_moment, row_weight, col_weight):
    dp_count = lax.axis_size("dp")
    pipe_count = lax.axis_size("pipe")
    tensor_count = lax.axis_size("tensor")
    shard_rows, width = weights.shape
    dp_section = dp_count // pipe_count
    tile_shards = dp_count // tensor_count
    piece_cols = width // dp_count
    tile_rows = shard_rows * dp_count
    col_blocks = width // CHECK_COLS
    factor = float(tile_rows * CHECK_COLS) ** (-0.5)
    sources = (weights, first_moment, second_moment)
    exchanged = (
        lax.all_to_all(sources[0], "dp", split_axis=1, concat_axis=0, tiled=True),
        lax.all_to_all(sources[1], "dp", split_axis=1, concat_axis=0, tiled=True),
        lax.all_to_all(sources[2], "dp", split_axis=1, concat_axis=0, tiled=True),
    )
    grouped = tuple(
        (item.reshape(pipe_count, dp_section, shard_rows, piece_cols) for item in exchanged)
    )
    sectioned = jax.tree.map(
        lambda part, own: part.astype(own.dtype),
        lax.all_to_all(for_sending(grouped), "pipe", split_axis=0, concat_axis=2, tiled=True),
        grouped,
    )
    routed = tuple(
        (item.reshape(tensor_count, tile_shards, 1, shard_rows, piece_cols) for item in sectioned)
    )
    arrived = jax.tree.map(
        lambda part, own: part.astype(own.dtype),
        lax.all_to_all(for_sending(routed), "tensor", split_axis=0, concat_axis=2, tiled=True),
        routed,
    )
    flat_pieces = tuple((item.reshape(tile_rows, piece_cols) for item in arrived))
    tiles = jax.tree.map(
        lambda part, own: part.astype(own.dtype),
        lax.all_gather(for_sending(flat_pieces), "dp", axis=1, tiled=True),
        flat_pieces,
    )
    tensor_pos = lax.axis_index("tensor")
    flat_index = (
        lax.axis_index("dp") * pipe_count + lax.axis_index("pipe")
    ) * tensor_count + tensor_pos
    in_section = flat_index % (dp_count * tensor_count)
    section_of = flat_index // (dp_count * tensor_count)
    tile_of = in_section // dp_count
    row_part = lax.dynamic_slice_in_dim(row_weight, in_section * shard_rows, shard_rows)
    partial_value = jnp.stack(
        [column_sums(item, row_part, col_weight, col_blocks) for item in sources]
    )
    section_hit = (jnp.arange(pipe_count) == section_of).astype(jnp.float32)
    tile_hit = (jnp.arange(tensor_count) == tile_of).astype(jnp.float32)
    spread = (
        partial_value[:, None, None, :]
        * section_hit[None, :, None, None]
        * tile_hit[None, None, :, None]
    )
    summed = lax.psum(spread, ("dp", "pipe", "tensor"))
    checks = (
        lax.dynamic_slice(summed, (0, lax.axis_index("pipe"), tensor_pos, 0), (3, 1, 1, col_blocks))
        * factor
    )
    return (tiles[0], tiles[1], tiles[2], checks)


def solution(mesh):
    return jax.shard_map(
        shards,
        mesh=mesh,
        in_specs=(
            P(("dp", "pipe", "tensor"), None),
            P(("dp", "pipe", "tensor"), None),
            P(("dp", "pipe", "tensor"), None),
            P(),
            P(),
        ),
        out_specs=(
            P(("pipe", "tensor"), None),
            P(("pipe", "tensor"), None),
            P(("pipe", "tensor"), None),
            P(None, "pipe", "tensor", None),
        ),
        check_vma=False,
    )
```

profile of v0, /device:TPU:0, one launch (start us, length us, event | category | flops | bytes accessed | tf_op | source)
XLA Modules:
  0.0 154.1 jit_solution(8427268718347811385)
XLA Ops:
  0.7 1.3 all_to_all.90
  1.9 0.7 copy.33
  2.7 4.4 %all-to-all-start = ((bf16[88,4,352]{2,0,1:T(8,128)(2,1)}), bf16[88,4,352]{2,0,1:T(8,128)(2,1)}, u32[]{:S(2)}, u32[]{:S(2)}) async-start(bf16[88,4,352]{2,0,1:T(8,128)(2,1)} %copy.33), calls=%async_computation | async-start | bytes 540672 | tf_op jit(solution)/shard_map/all_to_all | solution.py:33
  7.3 0.7 copy.37
  8.1 5.6 %all-to-all-done = bf16[88,4,352]{2,0,1:T(8,128)(2,1)} async-done(((bf16[88,4,352]{2,0,1:T(8,128)(2,1)}), bf16[88,4,352]{2,0,1:T(8,128)(2,1)}, u32[]{:S(2)}, u32[]{:S(2)}) %all-to-all-start) | async-done | bytes 247840 | tf_op jit(solution)/shard_map/all_to_all | solution.py:33
  13.7 4.1 %all-to-all-start.3 = ((bf16[88,4,352]{2,0,1:T(8,128)(2,1)}), bf16[88,4,352]{2,0,1:T(8,128)(2,1)}, u32[]{:S(2)}, u32[]{:S(2)}) async-start(bf16[88,4,352]{2,0,1:T(8,128)(2,1)} %copy.37), calls=%async_computation.3 | async-start | bytes 540672 | tf_op jit(solution)/shard_map/all_to_all | solution.py:34
  18.1 0.7 copy.41
  18.9 5.1 %all-to-all-done.3 = bf16[88,4,352]{2,0,1:T(8,128)(2,1)} async-done(((bf16[88,4,352]{2,0,1:T(8,128)(2,1)}), bf16[88,4,352]{2,0,1:T(8,128)(2,1)}, u32[]{:S(2)}, u32[]{:S(2)}) %all-to-all-start.3) | async-done | bytes 247840 | tf_op jit(solution)/shard_map/all_to_all | solution.py:34
  24.0 4.1 %all-to-all-start.6 = ((bf16[88,4,352]{2,0,1:T(8,128)(2,1)}), bf16[88,4,352]{2,0,1:T(8,128)(2,1)}, u32[]{:S(2)}, u32[]{:S(2)}) async-start(bf16[88,4,352]{2,0,1:T(8,128)(2,1)} %copy.41), calls=%async_computation.6 | async-start | bytes 540672 | tf_op jit(solution)/shard_map/all_to_all | solution.py:35
  28.1 0.3 convolution_reduce_fusion.2
  28.4 0.3 convolution_reduce_fusion
  28.7 5.5 %all-to-all-done.6 = bf16[88,4,352]{2,0,1:T(8,128)(2,1)} async-done(((bf16[88,4,352]{2,0,1:T(8,128)(2,1)}), bf16[88,4,352]{2,0,1:T(8,128)(2,1)}, u32[]{:S(2)}, u32[]{:S(2)}) %all-to-all-start.6) | async-done | bytes 247840 | tf_op jit(solution)/shard_map/all_to_all | solution.py:35
  34.2 3.6 %all-to-all-start.1 = ((bf16[2,2,88,352]{3,2,1,0:T(8,128)(2,1)}), bf16[2,2,88,352]{3,2,1,0:T(8,128)(2,1)S(1)}, u32[]{:S(2)}, u32[]{:S(2)}) async-start(bf16[2,2,88,352]{3,2,1,0:T(8,128)(2,1)} %bitcast.1), calls=%async_computation.1 | async-start | bytes 540672 | tf_op jit(solution)/shard_map/all_to_all | solution.py:42
  38.3 5.2 %all-to-all-done.1 = bf16[2,2,88,352]{3,2,1,0:T(8,128)(2,1)S(1)} async-done(((bf16[2,2,88,352]{3,2,1,0:T(8,128)(2,1)}), bf16[2,2,88,352]{3,2,1,0:T(8,128)(2,1)S(1)}, u32[]{:S(2)}, u32[]{:S(2)}) %all-to-all-start.1) | async-done | bytes 247840 | tf_op jit(solution)/shard_map/all_to_all | solution.py:42
  43.5 3.4 %all-to-all-start.4 = ((bf16[2,2,88,352]{3,2,1,0:T(8,128)(2,1)}), bf16[2,2,88,352]{3,2,1,0:T(8,128)(2,1)S(1)}, u32[]{:S(2)}, u32[]{:S(2)}) async-start(bf16[2,2,88,352]{3,2,1,0:T(8,128)(2,1)} %bitcast.8), calls=%async_computation.4 | async-start | bytes 540672 | tf_op jit(solution)/shard_map/all_to_all | solution.py:42
  47.0 5.2 %all-to-all-done.4 = bf16[2,2,88,352]{3,2,1,0:T(8,128)(2,1)S(1)} async-done(((bf16[2,2,88,352]{3,2,1,0:T(8,128)(2,1)}), bf16[2,2,88,352]{3,2,1,0:T(8,128)(2,1)S(1)}, u32[]{:S(2)}, u32[]{:S(2)}) %all-to-all-start.4) | async-done | bytes 247840 | tf_op jit(solution)/shard_map/all_to_all | solution.py:42
  52.1 3.4 %all-to-all-start.7 = ((bf16[2,2,88,352]{3,2,1,0:T(8,128)(2,1)}), bf16[2,2,88,352]{3,2,1,0:T(8,128)(2,1)S(1)}, u32[]{:S(2)}, u32[]{:S(2)}) async-start(bf16[2,2,88,352]{3,2,1,0:T(8,128)(2,1)} %bitcast.15), calls=%async_computation.7 | async-start | bytes 540672 | tf_op jit(solution)/shard_map/all_to_all | solution.py:42
  55.6 0.7 copy.34
  56.4 4.4 %all-to-all-done.7 = bf16[2,2,88,352]{3,2,1,0:T(8,128)(2,1)S(1)} async-done(((bf16[2,2,88,352]{3,2,1,0:T(8,128)(2,1)}), bf16[2,2,88,352]{3,2,1,0:T(8,128)(2,1)S(1)}, u32[]{:S(2)}, u32[]{:S(2)}) %all-to-all-start.7) | async-done | bytes 247840 | tf_op jit(solution)/shard_map/all_to_all | solution.py:42
  60.8 5.1 %all-to-all-start.2 = ((bf16[4,1,1,88,352]{4,3,2,1,0:T(8,128)(2,1)}), bf16[4,1,1,88,352]{4,3,2,1,0:T(8,128)(2,1)S(1)}, u32[]{:S(2)}, u32[]{:S(2)}) async-start(bf16[4,1,1,88,352]{4,3,2,1,0:T(8,128)(2,1)} %bitcast.5), calls=%async_computation.2 | async-start | bytes 540672 | tf_op jit(solution)/shard_map/all_to_all | solution.py:50
  65.9 39.9 %psum.7 = f32[3,2,4,11]{3,2,1,0:T(4,128)S(1)} all-reduce(f32[3,2,4,11]{3,2,1,0:T(4,128)S(1)} %broadcast_multiply_fusion), channel_id=1, replica_groups=mesh['dp'=4,'pipe'=2,'tensor'=4] {'dp','pipe','tensor'}, use_global_device_ids=true, to_apply=%region_3.4 | all-reduce | flops 264 | bytes 2112 | tf_op jit(solution)/shard_map/psum | solution.py:77
  105.8 0.6 dynamic-slice_multiply_fusion
  106.4 0.7 copy.38
  107.1 0.7 copy.42
  107.9 3.6 %all-to-all-start.5 = ((bf16[4,1,1,88,352]{4,3,2,1,0:T(8,128)(2,1)}), bf16[4,1,1,88,352]{4,3,2,1,0:T(8,128)(2,1)S(1)}, u32[]{:S(2)}, u32[]{:S(2)}) async-start(bf16[4,1,1,88,352]{4,3,2,1,0:T(8,128)(2,1)} %bitcast.12), calls=%async_computation.5 | async-start | bytes 540672 | tf_op jit(solution)/shard_map/all_to_all | solution.py:50
  111.6 11.0 %all_gather.9 = bf16[352,1408]{0,1:T(8,128)(2,1)S(1)} all-gather(bf16[352,352]{0,1:T(8,128)(2,1)S(1)} %copy.36), channel_id=1, replica_groups=mesh['dp'=4,'pipe'=2,'tensor'=4] {'dp'}, dimensions={1}, use_global_device_ids=true | all-gather | bytes 1239040 | tf_op jit(solution)/shard_map/all_gather | solution.py:56
  122.6 1.9 %copy.45 = bf16[352,1408]{1,0:T(8,128)(2,1)} copy(bf16[352,1408]{0,1:T(8,128)(2,1)S(1)} %all_gather.9) | data formatting | bytes 1982464
  124.5 5.1 %all-to-all-start.8 = ((bf16[4,1,1,88,352]{4,3,2,1,0:T(8,128)(2,1)}), bf16[4,1,1,88,352]{4,3,2,1,0:T(8,128)(2,1)S(1)}, u32[]{:S(2)}, u32[]{:S(2)}) async-start(bf16[4,1,1,88,352]{4,3,2,1,0:T(8,128)(2,1)} %bitcast.19), calls=%async_computation.8 | async-start | bytes 540672 | tf_op jit(solution)/shard_map/all_to_all | solution.py:50
  129.8 10.0 %all_gather.10 = bf16[352,1408]{0,1:T(8,128)(2,1)S(1)} all-gather(bf16[352,352]{0,1:T(8,128)(2,1)S(1)} %copy.40), channel_id=1, replica_groups=mesh['dp'=4,'pipe'=2,'tensor'=4] {'dp'}, dimensions={1}, use_global_device_ids=true | all-gather | bytes 1239040 | tf_op jit(solution)/shard_map/all_gather | solution.py:56
  139.8 1.9 %copy.46 = bf16[352,1408]{1,0:T(8,128)(2,1)} copy(bf16[352,1408]{0,1:T(8,128)(2,1)S(1)} %all_gather.10) | data formatting | bytes 1982464
  141.9 10.3 %all_gather.11 = bf16[352,1408]{0,1:T(8,128)(2,1)S(1)} all-gather(bf16[352,352]{0,1:T(8,128)(2,1)S(1)} %copy.44), channel_id=1, replica_groups=mesh['dp'=4,'pipe'=2,'tensor'=4] {'dp'}, dimensions={1}, use_global_device_ids=true | all-gather | bytes 1239040 | tf_op jit(solution)/shard_map/all_gather | solution.py:56
  152.2 1.9 %copy.47 = bf16[352,1408]{1,0:T(8,128)(2,1)} copy(bf16[352,1408]{0,1:T(8,128)(2,1)S(1)} %all_gather.11) | data formatting | bytes 1982464
  (25 shorter events, 1.8 us)
Async XLA Ops:
  0.6 27.4 %copy-start = (f32[1408]{0:T(1024)S(1)}, f32[1408]{0:T(1024)}, u32[]{:S(2)}) copy-start(f32[1408]{0:T(1024)} %param.8) | copy-start | bytes 16900
  0.6 6.4 %copy-start.3 = (bf16[88,1408]{1,0:T(8,128)(2,1)S(1)}, bf16[88,1408]{1,0:T(8,128)(2,1)}, u32[]{:S(2)}) copy-start(bf16[88,1408]{1,0:T(8,128)(2,1)} %param.6) | copy-start | bytes 743428
  2.7 15.2 %copy-start.2 = (bf16[88,1408]{1,0:T(8,128)(2,1)S(1)}, bf16[88,1408]{1,0:T(8,128)(2,1)}, u32[]{:S(2)}) copy-start(bf16[88,1408]{1,0:T(8,128)(2,1)} %param.7) | copy-start | bytes 743428
  2.7 11.0 %all-to-all-start = ((bf16[88,4,352]{2,0,1:T(8,128)(2,1)}), bf16[88,4,352]{2,0,1:T(8,128)(2,1)}, u32[]{:S(2)}, u32[]{:S(2)}) async-start(bf16[88,4,352]{2,0,1:T(8,128)(2,1)} %copy.33), calls=%async_computation | async-start | bytes 540672 | tf_op jit(solution)/shard_map/all_to_all | solution.py:33
  8.1 20.0 %copy-start.1 = (bf16[88,1408]{1,0:T(8,128)(2,1)S(1)}, bf16[88,1408]{1,0:T(8,128)(2,1)}, u32[]{:S(2)}) copy-start(bf16[88,1408]{1,0:T(8,128)(2,1)} %param.5) | copy-start | bytes 743428
  13.7 10.2 %all-to-all-start.3 = ((bf16[88,4,352]{2,0,1:T(8,128)(2,1)}), bf16[88,4,352]{2,0,1:T(8,128)(2,1)}, u32[]{:S(2)}, u32[]{:S(2)}) async-start(bf16[88,4,352]{2,0,1:T(8,128)(2,1)} %copy.37), calls=%async_computation.3 | async-start | bytes 540672 | tf_op jit(solution)/shard_map/all_to_all | solution.py:34
  18.1 20.0 %copy-start.4 = (f32[1408]{0:T(1024)S(1)}, f32[1408]{0:T(1024)}, u32[]{:S(2)}) copy-start(f32[1408]{0:T(1024)} %param.9) | copy-start | bytes 16900
  24.0 10.2 %all-to-all-start.6 = ((bf16[88,4,352]{2,0,1:T(8,128)(2,1)}), bf16[88,4,352]{2,0,1:T(8,128)(2,1)}, u32[]{:S(2)}, u32[]{:S(2)}) async-start(bf16[88,4,352]{2,0,1:T(8,128)(2,1)} %copy.41), calls=%async_computation.6 | async-start | bytes 540672 | tf_op jit(solution)/shard_map/all_to_all | solution.py:35
  34.2 9.3 %all-to-all-start.1 = ((bf16[2,2,88,352]{3,2,1,0:T(8,128)(2,1)}), bf16[2,2,88,352]{3,2,1,0:T(8,128)(2,1)S(1)}, u32[]{:S(2)}, u32[]{:S(2)}) async-start(bf16[2,2,88,352]{3,2,1,0:T(8,128)(2,1)} %bitcast.1), calls=%async_computation.1 | async-start | bytes 540672 | tf_op jit(solution)/shard_map/all_to_all | solution.py:42
  43.5 8.7 %all-to-all-start.4 = ((bf16[2,2,88,352]{3,2,1,0:T(8,128)(2,1)}), bf16[2,2,88,352]{3,2,1,0:T(8,128)(2,1)S(1)}, u32[]{:S(2)}, u32[]{:S(2)}) async-start(bf16[2,2,88,352]{3,2,1,0:T(8,128)(2,1)} %bitcast.8), calls=%async_computation.4 | async-start | bytes 540672 | tf_op jit(solution)/shard_map/all_to_all | solution.py:42
  52.1 8.7 %all-to-all-start.7 = ((bf16[2,2,88,352]{3,2,1,0:T(8,128)(2,1)}), bf16[2,2,88,352]{3,2,1,0:T(8,128)(2,1)S(1)}, u32[]{:S(2)}, u32[]{:S(2)}) async-start(bf16[2,2,88,352]{3,2,1,0:T(8,128)(2,1)} %bitcast.15), calls=%async_computation.7 | async-start | bytes 540672 | tf_op jit(solution)/shard_map/all_to_all | solution.py:42
  60.8 47.1 %all-to-all-start.2 = ((bf16[4,1,1,88,352]{4,3,2,1,0:T(8,128)(2,1)}), bf16[4,1,1,88,352]{4,3,2,1,0:T(8,128)(2,1)S(1)}, u32[]{:S(2)}, u32[]{:S(2)}) async-start(bf16[4,1,1,88,352]{4,3,2,1,0:T(8,128)(2,1)} %bitcast.5), calls=%async_computation.2 | async-start | bytes 540672 | tf_op jit(solution)/shard_map/all_to_all | solution.py:50
  107.9 16.6 %all-to-all-start.5 = ((bf16[4,1,1,88,352]{4,3,2,1,0:T(8,128)(2,1)}), bf16[4,1,1,88,352]{4,3,2,1,0:T(8,128)(2,1)S(1)}, u32[]{:S(2)}, u32[]{:S(2)}) async-start(bf16[4,1,1,88,352]{4,3,2,1,0:T(8,128)(2,1)} %bitcast.12), calls=%async_computation.5 | async-start | bytes 540672 | tf_op jit(solution)/shard_map/all_to_all | solution.py:50
  124.5 17.2 %all-to-all-start.8 = ((bf16[4,1,1,88,352]{4,3,2,1,0:T(8,128)(2,1)}), bf16[4,1,1,88,352]{4,3,2,1,0:T(8,128)(2,1)S(1)}, u32[]{:S(2)}, u32[]{:S(2)}) async-start(bf16[4,1,1,88,352]{4,3,2,1,0:T(8,128)(2,1)} %bitcast.19), calls=%async_computation.8 | async-start | bytes 540672 | tf_op jit(solution)/shard_map/all_to_all | solution.py:50
where the time goes:
time: 155 us; the launch traced here: 154 us
  blocking collectives  71.2 us (46%)
  starting transfers between devices  36.7 us (24%)
  waiting for transfers between devices  31 us (20%)
  local copies, waits for them, and re-layouts  12.5 us (8%)
    psum x1, blocking collectives, shards(): summed = lax.psum(spread, ('dp', 'pipe', 'tensor'))  39.9 us
    all_gather x3, blocking collectives, shards(): lax.all_gather(for_sending(flat_pieces), 'dp', axis=1, tiled=True)  31.3 us
    all_to_all x3, waiting for transfers between devices, shards(): lax.all_to_all(for_sending(grouped), 'pipe', split_axis=0, concat_axis=2,...  14.7 us
    all_to_all x3, starting transfers between devices, shards(): lax.all_to_all(for_sending(routed), 'tensor', split_axis=0, concat_axis=2...  13.7 us
    all_to_all x3, starting transfers between devices, shards(): lax.all_to_all(for_sending(grouped), 'pipe', split_axis=0, concat_axis=2,...  10.5 us
    unnamed x13, local copies, waits for them, and re-layouts  5.65 us
    all_to_all x1, waiting for transfers between devices, shards(): lax.all_to_all(sources[0], 'dp', split_axis=1, concat_axis=0, tiled=True)  5.65 us
    all_to_all x1, waiting for transfers between devices, shards(): lax.all_to_all(sources[2], 'dp', split_axis=1, concat_axis=0, tiled=True)  5.51 us
  transfers between devices with their start and end apart: 9, of which 6 were waited for; matrix products, arithmetic and copies ran while one was open for 6% of the time, Pallas kernels for 0%

commit v1 on v0

v1 whole, which is shorter than its diff:
```python
import jax
import jax.numpy as jnp
from jax import lax
from jax.sharding import PartitionSpec as P

CHECK_COLS = 128
AXES = ("dp", "pipe", "tensor")


def shard_moves(dp_count, pipe_count, tensor_count):
    moves = []
    for flat in range(dp_count * pipe_count * tensor_count):
        tile, shard = divmod(flat, dp_count)
        moves.append((flat, shard * pipe_count * tensor_count + tile))
    return moves


def column_sums(tile, row_part, col_weight, col_blocks):
    row_mixed = jnp.dot(
        row_part[None, :], tile.astype(jnp.float32), precision=lax.Precision.HIGHEST
    )[0]
    return jnp.sum((row_mixed * col_weight).reshape(col_blocks, -1), axis=1)


def shards(weights, first_moment, second_moment, row_weight, col_weight):
    dp_count = lax.axis_size("dp")
    pipe_count = lax.axis_size("pipe")
    tensor_count = lax.axis_size("tensor")
    shard_rows, width = weights.shape
    tile_rows = shard_rows * dp_count
    col_blocks = width // CHECK_COLS
    factor = float(tile_rows * CHECK_COLS) ** (-0.5)
    moves = shard_moves(dp_count, pipe_count, tensor_count)
    arrived = [
        lax.ppermute(item, AXES, moves) for item in (weights, first_moment, second_moment)
    ]
    tiles = [lax.all_gather(item, "dp", axis=0, tiled=True) for item in arrived]
    row_part = lax.dynamic_slice_in_dim(
        row_weight, lax.axis_index("tensor") * tile_rows, tile_rows
    )
    checks = jnp.stack([column_sums(tile, row_part, col_weight, col_blocks) for tile in tiles])
    return (*tiles, checks[:, None, None, :] * factor)


def solution(mesh):
    return jax.shard_map(
        shards,
        mesh=mesh,
        in_specs=(P(AXES, None), P(AXES, None), P(AXES, None), P(), P()),
        out_specs=(
            P(("pipe", "tensor"), None),
            P(("pipe", "tensor"), None),
            P(("pipe", "tensor"), None),
            P(None, "pipe", "tensor", None),
        ),
        check_vma=False,
    )
```

time: 155 us -> 61.3 us (0.40)
  starting transfers between devices: 36.7 us -> 4.78 us
  waiting for transfers between devices: 31 us -> 0.01 us
  blocking collectives: 71.2 us -> 49.5 us
  local copies, waits for them, and re-layouts: 12.5 us -> 3.79 us
    psum x1 -> x0, blocking collectives: 39.9 us -> none  [shards(): summed = lax.psum(spread, ('dp', 'pipe', 'tensor'))]
    all_to_all x9 -> x0, starting transfers between devices: 36.7 us -> none  [the longest x3 13.7 us: shards(): lax.all_to_all(for_sending(routed), 'tensor', split_axis=0, concat_axis=2...]
    all_to_all x9 -> x0, waiting for transfers between devices: 31 us -> none  [the longest x3 14.7 us: shards(): lax.all_to_all(for_sending(grouped), 'pipe', split_axis=0, concat_axis=2,...]
    all_gather x3, blocking collectives: 31.3 us -> 49.5 us  [shards(): tiles = [lax.all_gather(item, 'dp', axis=0, tiled=True) for item in arrived]]
    all_to_all x9 -> x0, local copies, waits for them, and re-layouts: 6.22 us -> none  [the longest x3 2.18 us: shards(): lax.all_to_all(for_sending(grouped), 'pipe', split_axis=0, concat_axis=2,...]
    ppermute x0 -> x3, starting transfers between devices: none -> 4.78 us  [shards(): lax.ppermute(item, AXES, moves)]
    unnamed x13 -> x5, local copies, waits for them, and re-layouts: 5.65 us -> 3.02 us
  transfers between devices with their start and end apart: 9 -> 3, of which waited for: 6 -> 0; matrix products, arithmetic and copies ran while one was open for 6% -> 3% of each run, Pallas kernels for 0% -> 0%
where the time goes in v1:
time: 61.3 us; the launch traced here: 61 us
  blocking collectives  49.5 us (81%)
  starting transfers between devices  4.78 us (8%)
  local copies, waits for them, and re-layouts  3.79 us (6%)
  matrix products  1.55 us (3%)
  other arithmetic  0.72 us (1%)
  between operations  0.65 us (1%)
    all_gather x3, blocking collectives, shards(): tiles = [lax.all_gather(item, 'dp', axis=0, tiled=True) for item in arrived]  49.5 us
    ppermute x3, starting transfers between devices, shards(): lax.ppermute(item, AXES, moves)  4.78 us
    unnamed x5, local copies, waits for them, and re-layouts  3.02 us
    dot_general x3, matrix products, column_sums(): jnp.dot(row_part[None, :], tile.astype(jnp.float32), precision=lax.Precis...  1.55 us
  transfers between devices with their start and end apart: 3, of which 0 were waited for; matrix products, arithmetic and copies ran while one was open for 3% of the time, Pallas kernels for 0%

profile of v1, /device:TPU:0, one launch (start us, length us, event | category | flops | bytes accessed | tf_op | source)
XLA Modules:
  0.0 61.0 jit_solution(5176911618751808828)
XLA Ops:
  0.6 1.6 %collective-permute-start.2 = (bf16[88,1408]{1,0:T(8,128)(2,1)}, bf16[88,1408]{1,0:T(8,128)(2,1)S(1)}, u32[]{:S(2)}, u32[]{:S(2)}) collective-permute-start(bf16[88,1408]{1,0:T(8,128)(2,1)} %param.7), channel_id=1, source_target_pairs={{0,0},{1,8},{2,16},{3,24},{4,1},{5,9},{6,17},{7,25},{8,2},{9,10},{... | collective-permute-start | bytes 743432 | tf_op jit(solution)/shard_map/ppermute | solution.py:35
  2.2 1.6 %collective-permute-start = (bf16[88,1408]{1,0:T(8,128)(2,1)}, bf16[88,1408]{1,0:T(8,128)(2,1)S(1)}, u32[]{:S(2)}, u32[]{:S(2)}) collective-permute-start(bf16[88,1408]{1,0:T(8,128)(2,1)} %param.5), channel_id=1, source_target_pairs={{0,0},{1,8},{2,16},{3,24},{4,1},{5,9},{6,17},{7,25},{8,2},{9,10},{... | collective-permute-start | bytes 743432 | tf_op jit(solution)/shard_map/ppermute | solution.py:35
  3.8 1.6 %collective-permute-start.1 = (bf16[88,1408]{1,0:T(8,128)(2,1)}, bf16[88,1408]{1,0:T(8,128)(2,1)S(1)}, u32[]{:S(2)}, u32[]{:S(2)}) collective-permute-start(bf16[88,1408]{1,0:T(8,128)(2,1)} %param.6), channel_id=1, source_target_pairs={{0,0},{1,8},{2,16},{3,24},{4,1},{5,9},{6,17},{7,25},{8,2},{9,10},{... | collective-permute-start | bytes 743432 | tf_op jit(solution)/shard_map/ppermute | solution.py:35
  5.4 0.8 %dynamic_slice.3 = f32[352]{0:T(512)S(1)} dynamic-slice(f32[1408]{0:T(1024)} %param.8, s32[]{:T(128)S(6)} %select_n.3), dynamic_slice_sizes={352} | dynamic-slice | bytes 2820 | tf_op jit(solution)/shard_map/dynamic_slice | solution.py:38
  6.2 0.0 collective-permute-done.2
  6.2 30.0 %all_gather.11 = bf16[352,1408]{1,0:T(8,128)(2,1)S(1)} all-gather(bf16[88,1408]{1,0:T(8,128)(2,1)S(1)} %collective-permute-done.2), channel_id=1, replica_groups=mesh['dp'=4,'pipe'=2,'tensor'=4] {'dp'}, dimensions={0}, use_global_device_ids=true | all-gather | bytes 1239040 | tf_op jit(solution)/shard_map/all_gather | solution.py:37
  36.2 0.0 collective-permute-done.1
  36.2 9.6 %all_gather.10 = bf16[352,1408]{1,0:T(8,128)(2,1)S(1)} all-gather(bf16[88,1408]{1,0:T(8,128)(2,1)S(1)} %collective-permute-done.1), channel_id=1, replica_groups=mesh['dp'=4,'pipe'=2,'tensor'=4] {'dp'}, dimensions={0}, use_global_device_ids=true | all-gather | bytes 1239040 | tf_op jit(solution)/shard_map/all_gather | solution.py:37
  45.8 0.5 convolution_reduce_fusion
  46.4 0.5 convolution_reduce_fusion.1
  46.9 0.0 collective-permute-done
  46.9 9.8 %all_gather.9 = bf16[352,1408]{1,0:T(8,128)(2,1)S(1)} all-gather(bf16[88,1408]{1,0:T(8,128)(2,1)S(1)} %collective-permute-done), channel_id=1, replica_groups=mesh['dp'=4,'pipe'=2,'tensor'=4] {'dp'}, dimensions={0}, use_global_device_ids=true | all-gather | bytes 1239040 | tf_op jit(solution)/shard_map/all_gather | solution.py:37
  56.7 0.0 copy-start
  56.7 0.5 convolution_reduce_fusion.2
  57.2 0.2 copy-done
  57.4 0.1 bitcast_reduce_fusion.2
  57.6 0.6 maximum_multiply_fusion
  58.1 0.9 %copy.12 = bf16[352,1408]{1,0:T(8,128)(2,1)} copy(bf16[352,1408]{1,0:T(8,128)(2,1)S(1)} %all_gather.9) | data formatting | bytes 1982464
  59.1 0.9 %copy.13 = bf16[352,1408]{1,0:T(8,128)(2,1)} copy(bf16[352,1408]{1,0:T(8,128)(2,1)S(1)} %all_gather.10) | data formatting | bytes 1982464
  60.0 0.9 %copy.14 = bf16[352,1408]{1,0:T(8,128)(2,1)} copy(bf16[352,1408]{1,0:T(8,128)(2,1)S(1)} %all_gather.11) | data formatting | bytes 1982464
  (1 shorter events, 0.0 us)
Async XLA Ops:
  0.6 5.6 %collective-permute-start.2 = (bf16[88,1408]{1,0:T(8,128)(2,1)}, bf16[88,1408]{1,0:T(8,128)(2,1)S(1)}, u32[]{:S(2)}, u32[]{:S(2)}) collective-permute-start(bf16[88,1408]{1,0:T(8,128)(2,1)} %param.7), channel_id=1, source_target_pairs={{0,0},{1,8},{2,16},{3,24},{4,1},{5,9},{6,17},{7,25},{8,2},{9,10},{... | collective-permute-start | bytes 743432 | tf_op jit(solution)/shard_map/ppermute | solution.py:35
  2.2 44.7 %collective-permute-start = (bf16[88,1408]{1,0:T(8,128)(2,1)}, bf16[88,1408]{1,0:T(8,128)(2,1)S(1)}, u32[]{:S(2)}, u32[]{:S(2)}) collective-permute-start(bf16[88,1408]{1,0:T(8,128)(2,1)} %param.5), channel_id=1, source_target_pairs={{0,0},{1,8},{2,16},{3,24},{4,1},{5,9},{6,17},{7,25},{8,2},{9,10},{... | collective-permute-start | bytes 743432 | tf_op jit(solution)/shard_map/ppermute | solution.py:35
  3.8 32.4 %collective-permute-start.1 = (bf16[88,1408]{1,0:T(8,128)(2,1)}, bf16[88,1408]{1,0:T(8,128)(2,1)S(1)}, u32[]{:S(2)}, u32[]{:S(2)}) collective-permute-start(bf16[88,1408]{1,0:T(8,128)(2,1)} %param.6), channel_id=1, source_target_pairs={{0,0},{1,8},{2,16},{3,24},{4,1},{5,9},{6,17},{7,25},{8,2},{9,10},{... | collective-permute-start | bytes 743432 | tf_op jit(solution)/shard_map/ppermute | solution.py:35
  56.7 0.7 %copy-start = (f32[1408]{0:T(1024)S(1)}, f32[1408]{0:T(1024)}, u32[]{:S(2)}) copy-start(f32[1408]{0:T(1024)} %param.9) | copy-start | bytes 16900
